TPU v7x, 128 devices: a whole 4x4x4 slice. The times are simulated.
128 devices in a mesh: row: 16 (over x, y), col: 8 (over z, core).
Axes of the slice: x: 4, y: 4, z: 4, core: 2. Of those that a mesh axis runs over, the one named last changes fastest.
Arguments:
- signal: float32 [256, 256, 16, 256], P('row', 'col'), may hold values from -40 to 40, as said below
- start_frames: float32 [256, 32], replicated, may hold values from -6 to 6
- start_sends: float32 [16, 8], replicated, may hold values from -6 to 6
- start_rows: float32 [256, 64], replicated, may hold values from -6 to 6
- start_cols: float32 [256, 64], replicated, may hold values from -6 to 6
- rank_frames: int32 [1], replicated, may hold values from 16 to 32
- rank_sends: int32 [1], replicated, may hold values from 4 to 8
Outputs:
- filtered: float32 [256, 256, 16, 256], P('row', 'col')
Inputs may be any that keep to these rules, and one draw needn't show every extreme that they name: `signal`: beamformed samples.
All inputs are finite; a program needn't handle non-finite values.
Results may differ from a plain program's by a relative error of at most 0.0003.
Values sent between devices are 32-bit elements; how exact they have to be, the bound alone decides.
A program may use at most 128 MiB of HBM per device.

v0:
```python
import jax
import jax.numpy as jnp
from jax import lax
from jax.sharding import Mesh
from jax.sharding import PartitionSpec as P

NT = 256
NK = 16
TMAX = 32
KMAX = 8
RS = 64
ITERS = 2
CORE_W = 256
ROW_COL = ("row_0", "row_1", "col_0", "col_1")
COL_ROW = ("col_0", "col_1", "row_0", "row_1")
COL = ("col_0", "col_1")
ROW = ("row_0", "row_1")


def split_up(shard, dim, size):
    dims = shard.shape
    pieces = shard.reshape(*dims[:dim], size, dims[dim] // size, *dims[dim + 1 :])
    return jnp.moveaxis(pieces, dim, 0)


def summed_on_arrival(shard, axis, dim):
    pieces = split_up(shard, dim, lax.axis_size(axis))
    arrived = lax.all_to_all(pieces, axis, split_axis=0, concat_axis=0, tiled=True)
    return arrived.sum(axis=0)


def summed_rows(shard, axes, dim):
    far, near = axes
    own = summed_on_arrival(split_up(shard, dim, lax.axis_size(far)), near, dim + 1)
    return jnp.sum(lax.all_to_all(own, far, 0, 0, tiled=True), axis=0)


def padded_to(lines, size):
    spare = -len(lines) % size
    return jnp.pad(lines, [(0, spare)] + [(0, 0)] * (lines.ndim - 1))


def copy_for_each(shard, axis):
    size = lax.axis_size(axis)
    return lax.all_to_all(
        jnp.broadcast_to(shard[None], (size, *shard.shape)), axis, 0, 0, tiled=True
    )


def laid_out(pieces, dim):
    dims = list(pieces.shape[1:])
    dims[dim] *= pieces.shape[0]
    return jnp.moveaxis(pieces, 0, dim).reshape(dims)


def whole_of(shard, axes, dim):
    far, near = axes
    first = copy_for_each(shard, far)
    pieces = jnp.swapaxes(copy_for_each(first, near), 0, 1)
    return laid_out(pieces.reshape(-1, *shard.shape), dim)


def sum_by_parts(shard, axes):
    own = summed_rows(padded_to(shard, lax.axis_size(axes[0]) * lax.axis_size(axes[1])), axes, 0)
    whole = whole_of(own, axes, 0)
    return whole[: len(shard)].reshape(shard.shape)


def in_one(arrays, axis):
    ends = [0]
    for a in arrays:
        ends.append(ends[-1] + a.size)
    subtotal = sum_by_parts(jnp.concatenate([a.ravel() for a in arrays]), axis)
    return tuple((subtotal[b:e].reshape(a.shape) for a, b, e in zip(arrays, ends, ends[1:])))


def one_exchange(shard, axis, axes, splits, concats):
    sizes = [lax.axis_size(a) for a in axes]
    pieces = split_up(shard, splits[0], sizes[0])
    pieces = jnp.moveaxis(split_up(pieces, splits[1] + 1, sizes[1]), 0, 1)
    inside = pieces.shape[2:]
    pieces = pieces.reshape(-1, *inside)
    pieces = lax.all_to_all(pieces, axis, split_axis=0, concat_axis=0, tiled=True)
    pieces = laid_out(pieces.reshape(*sizes, *inside), concats[0] + 1)
    return laid_out(pieces, concats[1])


def total_of(shard, axes):
    lines = shard.reshape(-1, shard.shape[-1])
    own = summed_rows(padded_to(lines, lax.axis_size(axes[0]) * lax.axis_size(axes[1])), axes, 0)
    whole = whole_of(own, axes, 0)
    return whole[: len(lines)].reshape(shard.shape)


def orthonormal(gram, start):
    high = lax.Precision.HIGHEST
    basis = start
    for rounds in range(ITERS):
        image = jnp.dot(gram, basis, precision=high)
        inner = jnp.dot(image.T, image, precision=high)
        factor = jnp.linalg.cholesky(inner)
        basis = jax.scipy.linalg.solve_triangular(factor, image.T, lower=True).T
    return basis


def local(signal, start_frames, start_sends, start_rows, start_cols, rank_frames, rank_sends):
    high = lax.Precision.HIGHEST
    rows_dev, cols_dev = (signal.shape[0], signal.shape[1])
    pixels = rows_dev * cols_dev
    flattened = signal.reshape(-1, NT)
    blocks = signal.reshape(pixels, NK, NT)
    local_frames = jnp.einsum("pt,pu->tu", flattened, flattened, precision=high)
    local_sends = jnp.einsum("pkt,pjt->kj", blocks, blocks, precision=high)
    gram_frames, gram_sends = in_one(
        (local_frames, local_sends), (("row_0", "row_1", "col_0"), "col_1")
    )
    keep_frames = (jnp.arange(TMAX, dtype=jnp.int32) < rank_frames[0]).astype(jnp.float32)
    keep_sends = (jnp.arange(KMAX, dtype=jnp.int32) < rank_sends[0]).astype(jnp.float32)
    basis_frames = orthonormal(gram_frames, start_frames) * keep_frames[None, :]
    basis_sends = orthonormal(gram_sends, start_sends) * keep_sends[None, :]
    reduced = jnp.dot(flattened, basis_frames, precision=high).reshape(pixels, NK, TMAX)
    core = jnp.einsum("pkb,ka->pab", reduced, basis_sends, precision=high)
    core = core.reshape(rows_dev, cols_dev, CORE_W)
    spread = one_exchange(core, COL_ROW, (COL, ROW), (2, 2), (1, 0))
    total_rows, total_cols = (spread.shape[0], spread.shape[1])
    unfolded = spread.reshape(total_rows, -1)
    local_rows = jnp.dot(unfolded, unfolded.T, precision=high)
    gram_rows = total_of(local_rows, (("row_0", "row_1", "col_0"), "col_1"))
    basis_rows = orthonormal(gram_rows, start_rows)
    second = jnp.dot(basis_rows.T, unfolded, precision=high).reshape(RS, total_cols, -1)
    local_cols = jnp.einsum("sce,sde->cd", second, second, precision=high)
    gram_cols = total_of(local_cols, (("row_0", "row_1", "col_0"), "col_1"))
    basis_cols = orthonormal(gram_cols, start_cols)
    third = jnp.einsum("cu,sce->sue", basis_cols, second, precision=high)
    back_cols = jnp.einsum("cu,sue->sce", basis_cols, third, precision=high)
    projected = jnp.dot(basis_rows, back_cols.reshape(RS, -1), precision=high).reshape(spread.shape)
    tissue_core = one_exchange(projected, ROW_COL, (ROW, COL), (0, 1), (2, 2))
    tissue_core = tissue_core.reshape(pixels, KMAX, TMAX)
    expanded = jnp.einsum("pab,ka->pkb", tissue_core, basis_sends, precision=high)
    tissue = jnp.dot(expanded.reshape(-1, TMAX), basis_frames.T, precision=high).reshape(
        signal.shape
    )
    return signal - tissue


def solution(mesh):
    finer = Mesh(mesh.devices.reshape(4, 4, 4, 2), ("row_0", "row_1", "col_0", "col_1"))
    return jax.shard_map(
        local,
        mesh=finer,
        in_specs=(P(ROW, COL, None, None), P(), P(), P(), P(), P(), P()),
        out_specs=P(ROW, COL, None, None),
        check_vma=False,
    )
```

profile of v0, /device:TPU:1, one launch (start us, length us, event | category | flops | bytes accessed | tf_op | source)
XLA Modules:
  0.0 369.9 jit_solution(14998686782036676919)
XLA Ops:
  0.0 17.4 %convolution_bitcast_fusion.5 = f32[32,2,8,128]{3,2,1,0:T(8,128)S(1)} fusion(f32[16,32,16,256]{3,2,1,0:T(8,128)} %param.16), kind=kOutput, calls=%fused_computation.6 | convolution fusion | flops 6442450944 | bytes 8650752 | tf_op jit(solution)/shard_map/pt,pu->tu/dot_general | solution.py:112
  17.4 11.4 %convolution_bitcast_fusion.9 = f32[16,16]{1,0:T(8,128)S(1)} fusion(f32[16,32,16,256]{3,2,1,0:T(8,128)S(1)} %copy-done.1), kind=kOutput, calls=%fused_computation.11 | convolution fusion | flops 402653184 | bytes 8389632 | tf_op jit(solution)/shard_map/pkt,pjt->kj/dot_general | solution.py:113
  29.5 5.0 %all_to_all.75 = f32[2,64,514]{2,1,0:T(8,128)S(1)} all-to-all(f32[2,64,514]{2,1,0:T(8,128)S(1)} %copy.167), channel_id=1, replica_groups=mesh['row_0'=4,'row_1'=4,'col_0'=4,'col_1'=2] {'col_1'}, dimensions={0} | all-to-all | bytes 526336 | tf_op jit(solution)/shard_map/all_to_all | solution.py:28
  35.3 11.2 %all-to-all-start.1 = ((f32[64,1,514]{2,1,0:T(1,128)}), f32[64,1,514]{2,1,0:T(1,128)S(1)}, u32[]{:S(2)}, u32[]{:S(2)}) async-start(f32[64,1,514]{2,1,0:T(1,128)} %all_to_all.47), calls=%async_computation.1 | async-start | bytes 327680 | tf_op jit(solution)/shard_map/all_to_all | solution.py:35
  47.2 8.1 %all-to-all-done.1 = f32[64,1,514]{2,1,0:T(1,128)S(1)} async-done(((f32[64,1,514]{2,1,0:T(1,128)}), f32[64,1,514]{2,1,0:T(1,128)S(1)}, u32[]{:S(2)}, u32[]{:S(2)}) %all-to-all-start.1) | async-done | bytes 131616 | tf_op jit(solution)/shard_map/all_to_all | solution.py:35
  56.2 5.1 %all-to-all-start.2 = ((f32[64,1,514]{2,1,0:T(1,128)}), f32[64,1,514]{2,1,0:T(1,128)S(1)}, u32[]{:S(2)}, u32[]{:S(2)}) async-start(f32[64,1,514]{2,1,0:T(1,128)} %broadcast_in_dim.16), calls=%async_computation.2 | async-start | bytes 327680 | tf_op jit(solution)/shard_map/all_to_all | solution.py:45
  62.0 8.1 %all-to-all-done.2 = f32[64,1,514]{2,1,0:T(1,128)S(1)} async-done(((f32[64,1,514]{2,1,0:T(1,128)}), f32[64,1,514]{2,1,0:T(1,128)S(1)}, u32[]{:S(2)}, u32[]{:S(2)}) %all-to-all-start.2) | async-done | bytes 131616 | tf_op jit(solution)/shard_map/all_to_all | solution.py:45
  70.2 6.9 %all_to_all.76 = f32[2,64,514]{2,1,0:T(8,128)S(1)} all-to-all(f32[2,64,514]{2,1,0:T(8,128)S(1)} %broadcast_in_dim.18), channel_id=1, replica_groups=mesh['row_0'=4,'row_1'=4,'col_0'=4,'col_1'=2] {'col_1'}, dimensions={0} | all-to-all | bytes 526336 | tf_op jit(solution)/shard_map/all_to_all | solution.py:45
  79.6 2.9 cholesky.180
  83.9 2.4 custom-call.22
  87.2 2.9 cholesky.191
  91.4 2.4 custom-call.23
  94.1 9.9 %convolution_bitcast_fusion = f32[8192,32]{0,1:T(8,128)S(1)} fusion(f32[32,256]{1,0:T(8,128)S(1)} %convolution_multiply_fusion, f32[8192,256]{1,0:T(8,128)} %bitcast.249), kind=kOutput, calls=%fused_computation | convolution fusion | flops 805306368 | bytes 9469952 | tf_op jit(solution)/shard_map/dot_general | solution.py:121
  104.0 2.7 copy.176
  106.7 3.2 copy.177
  117.6 1.5 copy.178
  119.2 2.5 reshape.119
  121.7 17.3 %all_to_all.77 = f32[128,1,1024]{2,1,0:T(1,128)S(1)} all-to-all(f32[128,1,1024]{2,1,0:T(1,128)S(1)} %reshape.119), channel_id=1, replica_groups=mesh['row_0'=4,'row_1'=4,'col_0'=4,'col_1'=2] {'col_0','col_1','row_0','..., dimensions={0} | all-to-all | bytes 1048576 | tf_op jit(solution)/shard_map/all_to_all | solution.py:83
  139.6 1.9 reduce.13
  142.2 18.3 %copy.179 = f32[16,16,8,32,2]{4,3,2,1,0:T(8,128)} copy(f32[16,16,8,32,2]{3,1,4,0,2:T(8,128)S(1)} %bitcast.250) | data formatting | bytes 1048576 | tf_op jit(solution)/shard_map/transpose | solution.py:53
  160.5 4.4 %copy.180 = f32[16,16,8,32,2]{1,0,4,3,2:T(8,128)} copy(f32[16,16,8,32,2]{3,1,4,0,2:T(8,128)S(1)} %bitcast.251) | data formatting | bytes 1048576 | tf_op jit(solution)/shard_map/transpose | solution.py:53
  164.9 24.5 %dot_general.115 = f32[64,2,2,512]{3,2,1,0:T(2,128)S(1)} reshape(f32[16,16,8,32,2]{4,3,2,1,0:T(8,128)} %copy.179) | data formatting | bytes 1048576 | tf_op jit(solution)/shard_map/dot_general | solution.py:127
  189.3 3.5 reshape_reshape_reshape.4
  193.5 4.9 %all_to_all.78 = f32[2,64,2,256]{3,1,2,0:T(8,128)S(1)} all-to-all(f32[2,64,2,256]{3,1,2,0:T(8,128)S(1)} %convolution_bitcast_fusion.3), channel_id=1, replica_groups=mesh['row_0'=4,'row_1'=4,'col_0'=4,'col_1'=2] {'col_1'}, dimensions={0} | all-to-all | bytes 524288 | tf_op jit(solution)/shard_map/all_to_all | solution.py:28
  198.5 12.9 %all_to_all.79 = f32[64,2,256]{2,1,0:T(2,128)S(1)} all-to-all(f32[64,2,256]{2,1,0:T(2,128)S(1)} %copy.183), channel_id=1, replica_groups=mesh['row_0'=4,'row_1'=4,'col_0'=4,'col_1'=2] {'row_0','row_1','col_0'}, dimensions={0} | all-to-all | bytes 262144 | tf_op jit(solution)/shard_map/all_to_all | solution.py:35
  212.2 5.0 %all-to-all-start.7 = ((f32[64,2,256]{2,1,0:T(2,128)}), f32[64,2,256]{2,1,0:T(2,128)S(1)}, u32[]{:S(2)}, u32[]{:S(2)}) async-start(f32[64,2,256]{2,1,0:T(2,128)} %broadcast_in_dim.19), calls=%async_computation.7 | async-start | bytes 262144 | tf_op jit(solution)/shard_map/all_to_all | solution.py:45
  217.6 8.3 %all-to-all-done.7 = f32[64,2,256]{2,1,0:T(2,128)S(1)} async-done(((f32[64,2,256]{2,1,0:T(2,128)}), f32[64,2,256]{2,1,0:T(2,128)S(1)}, u32[]{:S(2)}, u32[]{:S(2)}) %all-to-all-start.7) | async-done | bytes 131104 | tf_op jit(solution)/shard_map/all_to_all | solution.py:45
  226.0 6.7 %all_to_all.80 = f32[2,64,2,256]{3,2,1,0:T(2,128)S(1)} all-to-all(f32[2,64,2,256]{3,2,1,0:T(2,128)S(1)} %broadcast_in_dim.20), channel_id=1, replica_groups=mesh['row_0'=4,'row_1'=4,'col_0'=4,'col_1'=2] {'col_1'}, dimensions={0} | all-to-all | bytes 524288 | tf_op jit(solution)/shard_map/all_to_all | solution.py:45
  233.6 5.8 %cholesky.202 = f32[64,64]{1,0:T(8,128)S(1)} custom-call(f32[64,64]{1,0:T(8,128)S(1)} %fusion.32), custom_call_target="Cholesky" | custom-call | tf_op jit(solution)/shard_map/jit(cholesky)/cholesky | solution.py:101
  240.8 4.9 %custom-call.24 = f32[1,64,64]{1,2,0:T(8,128)S(1)} custom-call(f32[1,64,64]{2,1,0:T(8,128)S(1)} %fusion.20), custom_call_target="InvertDiagBlocksLowerTriangular" | custom-call | tf_op jit(solution)/shard_map/jit(_solve_triangular)/triangular_solve | solution.py:102
  246.7 5.8 %cholesky.213 = f32[64,64]{1,0:T(8,128)S(1)} custom-call(f32[64,64]{1,0:T(8,128)S(1)} %fusion.30), custom_call_target="Cholesky" | custom-call | tf_op jit(solution)/shard_map/jit(cholesky)/cholesky | solution.py:101
  253.9 4.9 %custom-call.25 = f32[1,64,64]{1,2,0:T(8,128)S(1)} custom-call(f32[1,64,64]{2,1,0:T(8,128)S(1)} %fusion.21), custom_call_target="InvertDiagBlocksLowerTriangular" | custom-call | tf_op jit(solution)/shard_map/jit(_solve_triangular)/triangular_solve | solution.py:102
  260.3 3.9 %all_to_all.81 = f32[2,64,2,256]{3,2,1,0:T(2,128)S(1)} all-to-all(f32[2,64,2,256]{3,2,1,0:T(2,128)S(1)} %bitcast.265), channel_id=1, replica_groups=mesh['row_0'=4,'row_1'=4,'col_0'=4,'col_1'=2] {'col_1'}, dimensions={0} | all-to-all | bytes 524288 | tf_op jit(solution)/shard_map/all_to_all | solution.py:28
  264.4 13.2 %all_to_all.82 = f32[64,2,256]{2,1,0:T(2,128)S(1)} all-to-all(f32[64,2,256]{2,1,0:T(2,128)S(1)} %reduce_sum.58), channel_id=1, replica_groups=mesh['row_0'=4,'row_1'=4,'col_0'=4,'col_1'=2] {'row_0','row_1','col_0'}, dimensions={0} | all-to-all | bytes 262144 | tf_op jit(solution)/shard_map/all_to_all | solution.py:35
  278.4 5.0 %all-to-all-start.11 = ((f32[64,2,256]{2,1,0:T(2,128)}), f32[64,2,256]{2,1,0:T(2,128)S(1)}, u32[]{:S(2)}, u32[]{:S(2)}) async-start(f32[64,2,256]{2,1,0:T(2,128)} %broadcast_in_dim.21), calls=%async_computation.11 | async-start | bytes 262144 | tf_op jit(solution)/shard_map/all_to_all | solution.py:45
  283.6 8.5 %all-to-all-done.11 = f32[64,2,256]{2,1,0:T(2,128)S(1)} async-done(((f32[64,2,256]{2,1,0:T(2,128)}), f32[64,2,256]{2,1,0:T(2,128)S(1)}, u32[]{:S(2)}, u32[]{:S(2)}) %all-to-all-start.11) | async-done | bytes 131104 | tf_op jit(solution)/shard_map/all_to_all | solution.py:45
  292.2 6.7 %all_to_all.83 = f32[2,64,2,256]{3,2,1,0:T(2,128)S(1)} all-to-all(f32[2,64,2,256]{3,2,1,0:T(2,128)S(1)} %broadcast_in_dim.22), channel_id=1, replica_groups=mesh['row_0'=4,'row_1'=4,'col_0'=4,'col_1'=2] {'col_1'}, dimensions={0} | all-to-all | bytes 524288 | tf_op jit(solution)/shard_map/all_to_all | solution.py:45
  299.9 5.8 %cholesky.224 = f32[64,64]{1,0:T(8,128)S(1)} custom-call(f32[64,64]{1,0:T(8,128)S(1)} %fusion.28), custom_call_target="Cholesky" | custom-call | tf_op jit(solution)/shard_map/jit(cholesky)/cholesky | solution.py:101
  307.0 4.9 %custom-call.26 = f32[1,64,64]{1,2,0:T(8,128)S(1)} custom-call(f32[1,64,64]{2,1,0:T(8,128)S(1)} %fusion.22), custom_call_target="InvertDiagBlocksLowerTriangular" | custom-call | tf_op jit(solution)/shard_map/jit(_solve_triangular)/triangular_solve | solution.py:102
  312.9 5.8 %cholesky.235 = f32[64,64]{1,0:T(8,128)S(1)} custom-call(f32[64,64]{1,0:T(8,128)S(1)} %fusion.26), custom_call_target="Cholesky" | custom-call | tf_op jit(solution)/shard_map/jit(cholesky)/cholesky | solution.py:101
  320.1 4.9 %custom-call.27 = f32[1,64,64]{1,2,0:T(8,128)S(1)} custom-call(f32[1,64,64]{2,1,0:T(8,128)S(1)} %fusion.23), custom_call_target="InvertDiagBlocksLowerTriangular" | custom-call | tf_op jit(solution)/shard_map/jit(_solve_triangular)/triangular_solve | solution.py:102
  325.9 1.8 fusion.5
  328.7 17.6 %all_to_all.84 = f32[128,1,1024]{2,1,0:T(1,128)S(1)} all-to-all(f32[128,1,1024]{2,1,0:T(1,128)S(1)} %reshape.121), channel_id=1, replica_groups=mesh['row_0'=4,'row_1'=4,'col_0'=4,'col_1'=2] {'row_0','row_1','col_0','..., dimensions={0} | all-to-all | bytes 1048576 | tf_op jit(solution)/shard_map/all_to_all | solution.py:83
  346.3 1.9 reduce.14
  348.9 1.6 copy.196
  350.5 2.3 reshape_reshape.25
  353.9 3.8 %copy.204 = f32[512,16,32]{2,1,0:T(8,128)} copy(f32[512,16,32]{0,1,2:T(8,128)S(1)} %convolution_bitcast_fusion.1) | data formatting | bytes 2097152 | tf_op jit(solution)/shard_map/dot_general | solution.py:140
  357.7 11.7 %convolution_subtract_fusion = f32[16,32,16,256]{3,2,1,0:T(8,128)} fusion(f32[16,32,16,256]{3,2,1,0:T(8,128)} %param.16, f32[16,32,16,32]{3,2,1,0:T(8,128)} %bitcast.252, f32[32,256]{1,0:T(8,128)S(1)} %convolution_multiply_fusion), kind=kOutput, calls=%fused_computation.1 | convolution fusion | flops 807403520 | bytes 17858560 | tf_op jit(solution)/shard_map/dot_general | solution.py:140
  (124 shorter events, 34.6 us)
Async XLA Ops:
  0.0 232.9 %copy-start = (f32[256,64]{0,1:T(8,128)S(1)}, f32[256,64]{0,1:T(8,128)}, u32[]{:S(2)}) copy-start(f32[256,64]{0,1:T(8,128)} %param.19) | copy-start | bytes 196612
  0.0 17.4 %copy-start.1 = (f32[16,32,16,256]{3,2,1,0:T(8,128)S(1)}, f32[16,32,16,256]{3,2,1,0:T(8,128)}, u32[]{:S(2)}) copy-start(f32[16,32,16,256]{3,2,1,0:T(8,128)} %param.16) | copy-start | bytes 25165828
  28.8 50.2 %copy-start.3 = (f32[256,32]{0,1:T(8,128)S(1)}, f32[256,32]{0,1:T(8,128)}, u32[]{:S(2)}) copy-start(f32[256,32]{0,1:T(8,128)} %param.17) | copy-start | bytes 98308
  35.3 20.0 %all-to-all-start.1 = ((f32[64,1,514]{2,1,0:T(1,128)}), f32[64,1,514]{2,1,0:T(1,128)S(1)}, u32[]{:S(2)}, u32[]{:S(2)}) async-start(f32[64,1,514]{2,1,0:T(1,128)} %all_to_all.47), calls=%async_computation.1 | async-start | bytes 327680 | tf_op jit(solution)/shard_map/all_to_all | solution.py:35
  56.2 13.9 %all-to-all-start.2 = ((f32[64,1,514]{2,1,0:T(1,128)}), f32[64,1,514]{2,1,0:T(1,128)S(1)}, u32[]{:S(2)}, u32[]{:S(2)}) async-start(f32[64,1,514]{2,1,0:T(1,128)} %broadcast_in_dim.16), calls=%async_computation.2 | async-start | bytes 327680 | tf_op jit(solution)/shard_map/all_to_all | solution.py:45
  94.1 15.8 %copy-start.4 = (f32[16,8]{0,1:T(8,128)S(1)}, f32[16,8]{0,1:T(8,128)}, u32[]{:S(2)}) copy-start(f32[16,8]{0,1:T(8,128)} %param.18) | copy-start | bytes 1540
  192.8 106.3 %copy-start.2 = (f32[256,64]{0,1:T(8,128)S(1)}, f32[256,64]{0,1:T(8,128)}, u32[]{:S(2)}) copy-start(f32[256,64]{0,1:T(8,128)} %param.20) | copy-start | bytes 196612
  212.2 13.7 %all-to-all-start.7 = ((f32[64,2,256]{2,1,0:T(2,128)}), f32[64,2,256]{2,1,0:T(2,128)S(1)}, u32[]{:S(2)}, u32[]{:S(2)}) async-start(f32[64,2,256]{2,1,0:T(2,128)} %broadcast_in_dim.19), calls=%async_computation.7 | async-start | bytes 262144 | tf_op jit(solution)/shard_map/all_to_all | solution.py:45
  278.4 13.7 %all-to-all-start.11 = ((f32[64,2,256]{2,1,0:T(2,128)}), f32[64,2,256]{2,1,0:T(2,128)S(1)}, u32[]{:S(2)}, u32[]{:S(2)}) async-start(f32[64,2,256]{2,1,0:T(2,128)} %broadcast_in_dim.21), calls=%async_computation.11 | async-start | bytes 262144 | tf_op jit(solution)/shard_map/all_to_all | solution.py:45
where the time goes:
time: 376 us; the launch traced here: 370 us
  blocking collectives  95.3 us (25%)
  local copies, waits for them, and re-layouts  79.3 us (21%)
  other arithmetic  71.4 us (19%)
  matrix products  61.8 us (16%)
  waiting for transfers between devices  33.2 us (9%)
  starting transfers between devices  26.4 us (7%)
    another operation x24, other arithmetic, orthonormal(): factor = jnp.linalg.cholesky(inner)  36.1 us
    all_to_all x2, blocking collectives, one_exchange(): lax.all_to_all(pieces, axis, split_axis=0, concat_axis=0, tiled=True)  35 us
    another operation x16, other arithmetic, orthonormal(): basis = jax.scipy.linalg.solve_triangular(factor, image.T, lower=True).T  30.9 us
    all_to_all x2, blocking collectives, summed_rows(): return jnp.sum(lax.all_to_all(own, far, 0, 0, tiled=True), axis=0)  26.2 us
    all_to_all x3, waiting for transfers between devices, copy_for_each(): lax.all_to_all(jnp.broadcast_to(shard[None], (size, *shard.shape)), axis,...  25 us
    dot_general x1, local copies, waits for them, and re-layouts, local(): local_rows = jnp.dot(unfolded, unfolded.T, precision=high)  24.5 us
    transpose x3, local copies, waits for them, and re-layouts, laid_out(): return jnp.moveaxis(pieces, 0, dim).reshape(dims)  24.3 us
    all_to_all x3, blocking collectives, copy_for_each(): lax.all_to_all(jnp.broadcast_to(shard[None], (size, *shard.shape)), axis,...  20.3 us
  transfers between devices with their start and end apart: 4, of which 4 were waited for; matrix products, arithmetic and copies ran while one was open for 0% of the time, Pallas kernels for 0%

commit v1 on v0

v1 whole, which is shorter than its diff:
```python
import functools

import jax
import jax.numpy as jnp
from jax import lax
from jax.experimental import pallas as pl
from jax.experimental.pallas import tpu as pltpu
from jax.sharding import PartitionSpec as P

NT = 256
NK = 16
TMAX = 32
KMAX = 8
RS = 64
ITERS = 2
CORE_W = 256
NDEV = 128
MESH = pl.DeviceIdType.MESH


def me_index():
    return lax.axis_index("row") * 8 + lax.axis_index("col")


def coords(dev):
    return (dev // 8, dev % 8)


def reduce_kernel(pieces, x_ref, g_ref, inbox, sem_out, sem_in, sem_out2, sem_in2):
    me = me_index()
    barrier = pltpu.get_barrier_semaphore()

    def greet(s, _):
        dev = (me + s) % NDEV
        pl.semaphore_signal(barrier, inc=1, device_id=coords(dev), device_id_type=MESH)
        return 0

    lax.fori_loop(1, NDEV, greet, 0)
    pl.semaphore_wait(barrier, NDEV - 1)

    chip = me // 2
    reducer = jnp.logical_and(me % 2 == 1, chip < pieces)
    first = chip % pieces

    def scatter(s, _):
        piece = (first + s) % pieces
        dev = 2 * piece + 1

        @pl.when(dev != me)
        def _():
            slot = (me - dev + 2 * NDEV - 1) % NDEV
            pltpu.make_async_remote_copy(
                src_ref=x_ref.at[piece],
                dst_ref=inbox.at[slot],
                send_sem=sem_out,
                recv_sem=sem_in,
                device_id=coords(dev),
                device_id_type=MESH,
            ).start()

        return 0

    lax.fori_loop(0, pieces, scatter, 0)

    @pl.when(reducer)
    def _():
        whole = inbox.at[pl.ds(0, NDEV - 1)]
        pltpu.make_async_copy(whole, whole, sem_in).wait()
        total = jnp.sum(inbox[...], axis=0) + x_ref[chip]
        g_ref[chip] = total

        def spread(s, _):
            dev = (me + s) % NDEV
            pltpu.make_async_remote_copy(
                src_ref=g_ref.at[chip],
                dst_ref=g_ref.at[chip],
                send_sem=sem_out2,
                recv_sem=sem_in2,
                device_id=coords(dev),
                device_id_type=MESH,
            ).start()
            return 0

        lax.fori_loop(1, NDEV, spread, 0)
        some = x_ref.at[pl.ds(0, pieces - 1)]
        pltpu.make_async_copy(some, some, sem_in2).wait()
        pltpu.make_async_copy(some, some, sem_out).wait()
        pltpu.make_async_copy(whole, whole, sem_out2).wait()

    @pl.when(jnp.logical_not(reducer))
    def _():
        every = x_ref.at[pl.ds(0, pieces)]
        pltpu.make_async_copy(every, every, sem_in2).wait()
        pltpu.make_async_copy(every, every, sem_out).wait()


def all_sum(tiles, ident):
    pieces = tiles.shape[0]
    return pl.pallas_call(
        functools.partial(reduce_kernel, pieces),
        out_shape=jax.ShapeDtypeStruct(tiles.shape, jnp.float32),
        in_specs=[pl.BlockSpec(memory_space=pltpu.VMEM)],
        out_specs=pl.BlockSpec(memory_space=pltpu.VMEM),
        scratch_shapes=[
            pltpu.VMEM((NDEV - 1, 8, 128), jnp.float32),
            pltpu.SemaphoreType.DMA,
            pltpu.SemaphoreType.DMA,
            pltpu.SemaphoreType.DMA,
            pltpu.SemaphoreType.DMA,
        ],
        compiler_params=pltpu.CompilerParams(collective_id=ident, has_side_effects=True),
        name=f"all_sum_{ident}",
    )(tiles)


def packed(gram):
    return jnp.concatenate(
        [gram[:128, :128].reshape(16, 8, 128), gram[:128, 128:].reshape(16, 8, 128), gram[128:, 128:].reshape(16, 8, 128)]
    )


def unpacked(tiles):
    a = tiles[:16].reshape(128, 128)
    b = tiles[16:32].reshape(128, 128)
    c = tiles[32:48].reshape(128, 128)
    return jnp.concatenate([jnp.concatenate([a, b], 1), jnp.concatenate([b.T, c], 1)], 0)


def orthonormal(gram, start):
    high = lax.Precision.HIGHEST
    basis = start
    for rounds in range(ITERS):
        image = jnp.dot(gram, basis, precision=high)
        inner = jnp.dot(image.T, image, precision=high)
        factor = jnp.linalg.cholesky(inner)
        basis = jax.scipy.linalg.solve_triangular(factor, image.T, lower=True).T
    return basis


def local(signal, start_frames, start_sends, start_rows, start_cols, rank_frames, rank_sends):
    high = lax.Precision.HIGHEST
    rows_dev, cols_dev = (signal.shape[0], signal.shape[1])
    pixels = rows_dev * cols_dev
    flattened = signal.reshape(-1, NT)
    blocks = signal.reshape(pixels, NK, NT)
    local_frames = jnp.einsum("pt,pu->tu", flattened, flattened, precision=high)
    local_sends = jnp.einsum("pkt,pjt->kj", blocks, blocks, precision=high)
    small = jnp.pad(local_sends, ((0, 0), (0, 112))).reshape(2, 8, 128)
    tiles = all_sum(jnp.concatenate([packed(local_frames), small]), 1)
    gram_frames = unpacked(tiles[:48])
    gram_sends = tiles[48:].reshape(16, 128)[:, :16]
    keep_frames = (jnp.arange(TMAX, dtype=jnp.int32) < rank_frames[0]).astype(jnp.float32)
    keep_sends = (jnp.arange(KMAX, dtype=jnp.int32) < rank_sends[0]).astype(jnp.float32)
    basis_frames = orthonormal(gram_frames, start_frames) * keep_frames[None, :]
    basis_sends = orthonormal(gram_sends, start_sends) * keep_sends[None, :]
    reduced = jnp.dot(flattened, basis_frames, precision=high).reshape(pixels, NK, TMAX)
    core = jnp.einsum("pkb,ka->pab", reduced, basis_sends, precision=high)
    core = core.reshape(rows_dev, cols_dev, CORE_W)
    parts = core.reshape(rows_dev, cols_dev, NDEV, 2).transpose(2, 0, 1, 3)
    spread = lax.all_to_all(parts, ("row", "col"), 0, 0, tiled=True)
    spread = spread.reshape(16, 8, rows_dev, cols_dev, 2).transpose(0, 2, 1, 3, 4).reshape(256, 256, 2)
    unfolded = spread.reshape(256, -1)
    local_rows = jnp.dot(unfolded, unfolded.T, precision=high)
    gram_rows = unpacked(all_sum(packed(local_rows), 2))
    basis_rows = orthonormal(gram_rows, start_rows)
    second = jnp.dot(basis_rows.T, unfolded, precision=high).reshape(RS, 256, -1)
    local_cols = jnp.einsum("sce,sde->cd", second, second, precision=high)
    gram_cols = unpacked(all_sum(packed(local_cols), 3))
    basis_cols = orthonormal(gram_cols, start_cols)
    third = jnp.einsum("cu,sce->sue", basis_cols, second, precision=high)
    back_cols = jnp.einsum("cu,sue->sce", basis_cols, third, precision=high)
    projected = jnp.dot(basis_rows, back_cols.reshape(RS, -1), precision=high).reshape(spread.shape)
    parts = projected.reshape(16, rows_dev, 8, cols_dev, 2).transpose(0, 2, 1, 3, 4).reshape(NDEV, rows_dev, cols_dev, 2)
    back = lax.all_to_all(parts, ("row", "col"), 0, 0, tiled=True)
    tissue_core = back.transpose(1, 2, 0, 3).reshape(pixels, KMAX, TMAX)
    expanded = jnp.einsum("pab,ka->pkb", tissue_core, basis_sends, precision=high)
    tissue = jnp.dot(expanded.reshape(-1, TMAX), basis_frames.T, precision=high).reshape(
        signal.shape
    )
    return signal - tissue


def solution(mesh):
    return jax.shard_map(
        local,
        mesh=mesh,
        in_specs=(P("row", "col", None, None), P(), P(), P(), P(), P(), P()),
        out_specs=P("row", "col", None, None),
        check_vma=False,
    )
```

time: 376 us -> 287 us (0.76)
  Pallas kernels: 0 us -> 72.8 us
  blocking collectives: 95.3 us -> 38.8 us
  local copies, waits for them, and re-layouts: 79.3 us -> 34.1 us
  waiting for transfers between devices: 33.2 us -> 0 us
  starting transfers between devices: 26.4 us -> 0 us
    pallas_call x0 -> x3, Pallas kernels: none -> 72.8 us  [all_sum(): pl.pallas_call(functools.partial(reduce_kernel, pieces), out_shape=jax.Sh...]
    all_to_all x10 -> x2, blocking collectives: 95.3 us -> 38.8 us  [the longest x1 19.7 us: local(): spread = lax.all_to_all(parts, ('row', 'col'), 0, 0, tiled=True)]
    all_to_all x4 -> x0, waiting for transfers between devices: 33.2 us -> none  [the longest x3 25 us: copy_for_each(): lax.all_to_all(jnp.broadcast_to(shard[None], (size, *shard.shape)), axis,...]
    all_to_all x4 -> x0, starting transfers between devices: 26.4 us -> none  [the longest x3 15.2 us: copy_for_each(): lax.all_to_all(jnp.broadcast_to(shard[None], (size, *shard.shape)), axis,...]
    dot_general x2 -> x1, local copies, waits for them, and re-layouts: 24.8 us -> 0.31 us  [local(): jnp.dot(basis_rows.T, unfolded, precision=high).reshape(RS, 256, -1)]
    transpose x8 -> x5, local copies, waits for them, and re-layouts: 26.2 us -> 2.07 us  [the longest x1 1.5 us: local(): tissue_core = back.transpose(1, 2, 0, 3).reshape(pixels, KMAX, TMAX)]
    reshape x1 -> x10, local copies, waits for them, and re-layouts: 0.08 us -> 10.2 us  [the longest x1 4.37 us: local(): spread.reshape(16, 8, rows_dev, cols_dev, 2).transpose(0, 2, 1, 3, 4)]
  transfers between devices with their start and end apart: 4 -> 0, of which waited for: 4 -> 0; matrix products, arithmetic and copies ran while one was open for 0% -> 0% of each run, Pallas kernels for 0% -> 0%
where the time goes in v1:
time: 287 us; the launch traced here: 283 us
  other arithmetic  72.9 us (25%)
  Pallas kernels  72.8 us (25%)
  matrix products  62.4 us (22%)
  blocking collectives  38.8 us (14%)
  local copies, waits for them, and re-layouts  34.1 us (12%)
    pallas_call x3, Pallas kernels, all_sum(): pl.pallas_call(functools.partial(reduce_kernel, pieces), out_shape=jax.Sh...  72.8 us
    another operation x24, other arithmetic, orthonormal(): factor = jnp.linalg.cholesky(inner)  36.1 us
    another operation x16, other arithmetic, orthonormal(): basis = jax.scipy.linalg.solve_triangular(factor, image.T, lower=True).T  30.9 us
    all_to_all x1, blocking collectives, local(): spread = lax.all_to_all(parts, ('row', 'col'), 0, 0, tiled=True)  19.7 us
    all_to_all x1, blocking collectives, local(): back = lax.all_to_all(parts, ('row', 'col'), 0, 0, tiled=True)  19 us
    dot_general x1, matrix products, local(): local_sends = jnp.einsum('pkt,pjt->kj', blocks, blocks, precision=high)  14.9 us
    dot_general x1, matrix products, local(): local_frames = jnp.einsum('pt,pu->tu', flattened, flattened, precision=high)  14 us
    dot_general x1, matrix products, local(): jnp.dot(expanded.reshape(-1, TMAX), basis_frames.T, precision=high)  11.7 us

profile of v1, /device:TPU:1, one launch (start us, length us, event | category | flops | bytes accessed | tf_op | source)
XLA Modules:
  0.0 283.0 jit_solution(13036338283339787315)
XLA Ops:
  0.0 14.9 %convolution_bitcast_fusion.8 = f32[16,16]{1,0:T(8,128)S(1)} fusion(f32[16,32,16,256]{3,2,1,0:T(8,128)} %param.16), kind=kOutput, calls=%fused_computation.10 | convolution fusion | flops 402653184 | bytes 8389632 | tf_op jit(solution)/shard_map/pkt,pjt->kj/dot_general | solution.py:147
  14.9 14.0 %convolution_bitcast_fusion.4 = f32[256,256]{1,0:T(8,128)S(1)} fusion(f32[16,32,16,256]{3,2,1,0:T(8,128)S(1)} %copy-done.1), kind=kOutput, calls=%fused_computation.5 | convolution fusion | flops 6442450944 | bytes 8650752 | tf_op jit(solution)/shard_map/pt,pu->tu/dot_general | solution.py:146
  29.0 0.7 pad_maximum_fusion.x_ref
  29.7 27.2 %all_sum_1.1 = f32[50,8,128]{2,1,0:T(8,128)} custom-call(f32[50,8,128]{2,1,0:T(8,128)} %pad_maximum_fusion.x_ref), custom_call_target="tpu_custom_call" | custom-call | tf_op jit(solution)/shard_map/all_sum_1/pallas_call | solution.py:99
  56.9 0.7 slice_bitcast_fusion.21
  57.6 0.9 slice_bitcast_fusion.14
  60.2 0.7 cholesky.158
  63.5 0.7 cholesky.169
  66.9 2.9 %cholesky.180 = f32[32,32]{1,0:T(8,128)S(1)} custom-call(f32[32,32]{1,0:T(8,128)S(1)} %fusion.44), custom_call_target="Cholesky" | custom-call | tf_op jit(solution)/shard_map/jit(cholesky)/cholesky | solution.py:135
  71.1 2.4 custom-call.22
  74.4 2.9 %cholesky.191 = f32[32,32]{1,0:T(8,128)S(1)} custom-call(f32[32,32]{1,0:T(8,128)S(1)} %fusion.42), custom_call_target="Cholesky" | custom-call | tf_op jit(solution)/shard_map/jit(cholesky)/cholesky | solution.py:135
  78.7 2.4 custom-call.23
  81.4 9.9 %convolution_bitcast_fusion = f32[8192,32]{0,1:T(8,128)S(1)} fusion(f32[32,256]{1,0:T(8,128)S(1)} %convolution_multiply_fusion, f32[8192,256]{1,0:T(8,128)} %bitcast.269), kind=kOutput, calls=%fused_computation | convolution fusion | flops 805306368 | bytes 9469952 | tf_op jit(solution)/shard_map/dot_general | solution.py:156
  91.2 2.7 copy.35
  93.9 3.2 %copy.36 = f32[512,16,32]{0,1,2:T(8,128)S(1)} copy(f32[512,16,32]{2,1,0:T(8,128)} %bitcast.271) | data formatting | bytes 2097152 | tf_op jit(solution)/shard_map/reshape | solution.py:156
  98.9 1.5 bitcast_bitcast_fusion.1
  100.4 2.5 reshape.156
  102.9 19.7 %all_to_all.10 = f32[128,1,1024]{2,1,0:T(1,128)S(1)} all-to-all(f32[128,1,1024]{2,1,0:T(1,128)S(1)} %reshape.156), channel_id=1, replica_groups=mesh['row'=16,'col'=8] {'row','col'}, dimensions={0} | all-to-all | bytes 1048576 | tf_op jit(solution)/shard_map/all_to_all | solution.py:160
  123.2 1.9 reduce.12
  125.0 0.7 reshape.157
  125.7 4.4 %copy.38 = f32[16,8,16,32,2]{2,0,4,3,1:T(8,128)} copy(f32[16,8,16,32,2]{3,2,4,1,0:T(8,128)S(1)} %bitcast.273) | data formatting | bytes 1048576 | tf_op jit(solution)/shard_map/reshape | solution.py:161
  130.1 3.5 %reshape_reshape.8 = f32[256,512]{0,1:T(8,128)S(1)} reshape(f32[16,16,8,32,2]{1,0,4,3,2:T(8,128)} %bitcast.272) | data formatting | bytes 1048576 | tf_op jit(solution)/shard_map/reshape;reshape | solution.py:162
  133.6 1.0 fusion.72
  134.7 0.7 pad_maximum_fusion.1.x_ref
  135.4 21.8 %all_sum_2.1 = f32[48,8,128]{2,1,0:T(8,128)} custom-call(f32[48,8,128]{2,1,0:T(8,128)} %pad_maximum_fusion.1.x_ref), custom_call_target="tpu_custom_call" | custom-call | tf_op jit(solution)/shard_map/all_sum_2/pallas_call | solution.py:99
  157.2 0.9 slice_bitcast_fusion.12
  158.9 5.8 %cholesky.202 = f32[64,64]{1,0:T(8,128)S(1)} custom-call(f32[64,64]{1,0:T(8,128)S(1)} %fusion.33), custom_call_target="Cholesky" | custom-call | tf_op jit(solution)/shard_map/jit(cholesky)/cholesky | solution.py:135
  166.1 4.9 %custom-call.24 = f32[1,64,64]{1,2,0:T(8,128)S(1)} custom-call(f32[1,64,64]{2,1,0:T(8,128)S(1)} %fusion.21), custom_call_target="InvertDiagBlocksLowerTriangular" | custom-call | tf_op jit(solution)/shard_map/jit(_solve_triangular)/triangular_solve | solution.py:136
  172.0 5.8 %cholesky.213 = f32[64,64]{1,0:T(8,128)S(1)} custom-call(f32[64,64]{1,0:T(8,128)S(1)} %fusion.31), custom_call_target="Cholesky" | custom-call | tf_op jit(solution)/shard_map/jit(cholesky)/cholesky | solution.py:135
  178.5 0.7 fusion.22
  179.1 4.9 %custom-call.25 = f32[1,64,64]{1,2,0:T(8,128)S(1)} custom-call(f32[1,64,64]{2,1,0:T(8,128)S(1)} %fusion.22), custom_call_target="InvertDiagBlocksLowerTriangular" | custom-call | tf_op jit(solution)/shard_map/jit(_solve_triangular)/triangular_solve | solution.py:136
  185.8 0.7 pad_maximum_fusion.2.x_ref
  186.5 23.7 %all_sum_3.1 = f32[48,8,128]{2,1,0:T(8,128)} custom-call(f32[48,8,128]{2,1,0:T(8,128)} %pad_maximum_fusion.2.x_ref), custom_call_target="tpu_custom_call" | custom-call | tf_op jit(solution)/shard_map/all_sum_3/pallas_call | solution.py:99
  210.2 0.9 slice_bitcast_fusion.10
  211.9 5.8 %cholesky.224 = f32[64,64]{1,0:T(8,128)S(1)} custom-call(f32[64,64]{1,0:T(8,128)S(1)} %fusion.29), custom_call_target="Cholesky" | custom-call | tf_op jit(solution)/shard_map/jit(cholesky)/cholesky | solution.py:135
  219.1 4.9 %custom-call.26 = f32[1,64,64]{1,2,0:T(8,128)S(1)} custom-call(f32[1,64,64]{2,1,0:T(8,128)S(1)} %fusion.23), custom_call_target="InvertDiagBlocksLowerTriangular" | custom-call | tf_op jit(solution)/shard_map/jit(_solve_triangular)/triangular_solve | solution.py:136
  225.0 5.8 %cholesky.235 = f32[64,64]{1,0:T(8,128)S(1)} custom-call(f32[64,64]{1,0:T(8,128)S(1)} %fusion.27), custom_call_target="Cholesky" | custom-call | tf_op jit(solution)/shard_map/jit(cholesky)/cholesky | solution.py:135
  232.2 4.9 %custom-call.27 = f32[1,64,64]{1,2,0:T(8,128)S(1)} custom-call(f32[1,64,64]{2,1,0:T(8,128)S(1)} %fusion.24), custom_call_target="InvertDiagBlocksLowerTriangular" | custom-call | tf_op jit(solution)/shard_map/jit(_solve_triangular)/triangular_solve | solution.py:136
  238.0 1.8 fusion.4
  239.8 0.9 reshape.158
  240.8 19.0 %all_to_all.11 = f32[128,1,1024]{2,1,0:T(1,128)S(1)} all-to-all(f32[128,1,1024]{2,1,0:T(1,128)S(1)} %reshape.158), channel_id=1, replica_groups=mesh['row'=16,'col'=8] {'row','col'}, dimensions={0} | all-to-all | bytes 1048576 | tf_op jit(solution)/shard_map/all_to_all | solution.py:174
  259.8 1.9 reduce.13
  261.6 0.7 reshape.159
  262.3 1.5 bitcast_bitcast_fusion
  263.8 2.3 reshape.146
  266.1 1.2 convolution_bitcast_fusion.1
  267.3 3.8 %copy.57 = f32[512,16,32]{2,1,0:T(8,128)} copy(f32[512,16,32]{0,1,2:T(8,128)S(1)} %convolution_bitcast_fusion.1) | data formatting | bytes 2097152 | tf_op jit(solution)/shard_map/dot_general | solution.py:177
  271.1 11.7 %convolution_subtract_fusion = f32[16,32,16,256]{3,2,1,0:T(8,128)} fusion(f32[16,32,16,256]{3,2,1,0:T(8,128)} %param.16, f32[16,32,16,32]{3,2,1,0:T(8,128)} %bitcast.270, f32[32,256]{1,0:T(8,128)S(1)} %convolution_multiply_fusion), kind=kOutput, calls=%fused_computation.1 | convolution fusion | flops 807403520 | bytes 17858560 | tf_op jit(solution)/shard_map/dot_general | solution.py:177
  (95 shorter events, 22.2 us)
Async XLA Ops:
  0.0 158.2 %copy-start = (f32[256,64]{0,1:T(8,128)S(1)}, f32[256,64]{0,1:T(8,128)}, u32[]{:S(2)}) copy-start(f32[256,64]{0,1:T(8,128)} %param.19) | copy-start | bytes 196612
  0.0 14.9 %copy-start.1 = (f32[16,32,16,256]{3,2,1,0:T(8,128)S(1)}, f32[16,32,16,256]{3,2,1,0:T(8,128)}, u32[]{:S(2)}) copy-start(f32[16,32,16,256]{3,2,1,0:T(8,128)} %param.16) | copy-start | bytes 25165828
  14.9 45.0 %copy-start.2 = (f32[16,8]{0,1:T(8,128)S(1)}, f32[16,8]{0,1:T(8,128)}, u32[]{:S(2)}) copy-start(f32[16,8]{0,1:T(8,128)} %param.18) | copy-start | bytes 1540
  14.9 51.3 %copy-start.4 = (f32[256,32]{0,1:T(8,128)S(1)}, f32[256,32]{0,1:T(8,128)}, u32[]{:S(2)}) copy-start(f32[256,32]{0,1:T(8,128)} %param.17) | copy-start | bytes 98308
  130.1 81.1 %copy-start.3 = (f32[256,64]{0,1:T(8,128)S(1)}, f32[256,64]{0,1:T(8,128)}, u32[]{:S(2)}) copy-start(f32[256,64]{0,1:T(8,128)} %param.20) | copy-start | bytes 196612

commit v2 on v1

v2 whole, which is shorter than its diff:
```python
import functools

import jax
import jax.numpy as jnp
from jax import lax
from jax.experimental import pallas as pl
from jax.experimental.pallas import tpu as pltpu
from jax.sharding import PartitionSpec as P

NT = 256
NK = 16
TMAX = 32
KMAX = 8
RS = 64
ITERS = 2
NDEV = 128
ROWS = 16
COLS = 32
LINES = COLS * NK
MESH = pl.DeviceIdType.MESH
F32 = jnp.float32
BF16 = jnp.bfloat16
HIGH = lax.Precision.HIGHEST


def me_index():
    return lax.axis_index("row") * 8 + lax.axis_index("col")


def coords(dev):
    return (dev // 8, dev % 8)


def dot(a, b, over=(1, 0)):
    dims = (((over[0],), (over[1],)), ((), ()))
    return lax.dot_general(a, b, dims, preferred_element_type=F32)


def full_dot(a, b, over=(1, 0)):
    dims = (((over[0],), (over[1],)), ((), ()))
    return lax.dot_general(a, b, dims, precision=HIGH, preferred_element_type=F32)


def halves(x):
    hi = x.astype(BF16)
    return hi, (x - hi.astype(F32)).astype(BF16)


def dot3(a, b, over=(1, 0)):
    a_hi, a_lo = halves(a)
    b_hi, b_lo = halves(b)
    return dot(a_hi, b_hi, over) + dot(a_hi, b_lo, over) + dot(a_lo, b_hi, over)


def self_dot(a):
    hi, lo = halves(a)
    side = dot(hi, lo, (1, 1))
    return dot(hi, hi, (1, 1)) + side + side.T


def remote(src, dst, send, recv, dev):
    return pltpu.make_async_remote_copy(
        src_ref=src, dst_ref=dst, send_sem=send, recv_sem=recv, device_id=coords(dev), device_id_type=MESH
    )


def wait_for(ref, count, sem):
    some = ref.at[pl.ds(0, count)]
    pltpu.make_async_copy(some, some, sem).wait()


def all_sum(me, pieces, part, inbox, total, sems):
    chip = me // 2
    reducer = jnp.logical_and(me % 2 == 1, chip < pieces)
    first = chip % pieces

    def scatter(s, _):
        piece = (first + s) % pieces
        dev = 2 * piece + 1

        @pl.when(dev != me)
        def _():
            slot = (me - dev + 2 * NDEV - 1) % NDEV
            remote(part.at[piece], inbox.at[slot], sems.at[0], sems.at[1], dev).start()

        return 0

    lax.fori_loop(0, pieces, scatter, 0)

    @pl.when(reducer)
    def _():
        wait_for(inbox, NDEV - 1, sems.at[1])
        lanes = [inbox[i] for i in range(4)]
        for i in range(4, NDEV - 1):
            lanes[i % 4] = lanes[i % 4] + inbox[i]
        total[chip] = (lanes[0] + lanes[1]) + (lanes[2] + lanes[3]) + part[chip]

        def spread(s, _):
            dev = (me + s) % NDEV
            remote(total.at[chip], total.at[chip], sems.at[2], sems.at[3], dev).start()
            return 0

        lax.fori_loop(1, NDEV, spread, 0)
        wait_for(part, pieces - 1, sems.at[3])
        wait_for(part, pieces - 1, sems.at[0])
        wait_for(inbox, NDEV - 1, sems.at[2])

    @pl.when(jnp.logical_not(reducer))
    def _():
        wait_for(part, pieces, sems.at[3])
        wait_for(part, pieces, sems.at[0])


def pack(gram, part):
    part[0:16] = gram[:128, :128].reshape(16, 8, 128)
    part[16:32] = gram[:128, 128:].reshape(16, 8, 128)
    part[32:48] = gram[128:, 128:].reshape(16, 8, 128)


def unpack(total, gram):
    corner = total[16:32].reshape(128, 128)
    gram[:128, :128] = total[0:16].reshape(128, 128)
    gram[:128, 128:] = corner
    gram[128:, :128] = corner.T
    gram[128:, 128:] = total[32:48].reshape(128, 128)


def inverse_factor(inner, size):
    groups = size // 8
    lane = lax.broadcasted_iota(jnp.int32, (8, 128), 1)
    sub = lax.broadcasted_iota(jnp.int32, (8, 128), 0)
    rest = [inner[8 * g : 8 * g + 8] for g in range(groups)]
    inv = [jnp.where(lane == sub + 8 * g, 1.0, 0.0).astype(F32) for g in range(groups)]

    def row(x, j):
        return jnp.broadcast_to(x[j : j + 1], (8, 128))

    for b in range(groups):
        cols = [
            [jnp.broadcast_to(rest[g][:, 8 * b + j : 8 * b + j + 1], (8, 128)) for g in range(b, groups)]
            for j in range(8)
        ]
        pivots = jnp.ones((8, 128), F32)
        for j in range(8):
            pivot = row(cols[j][0], j)
            pivots = jnp.where(sub == j, pivot, pivots)
            scale = 1.0 / pivot
            heads = [row(cols[q][0], j) for q in range(j + 1, 8)]
            rest_row = row(rest[b], j)
            inv_row = row(inv[b], j)
            for g in range(b, groups):
                step = cols[j][g - b] * scale
                if g == b:
                    step = jnp.where(sub > j, step, 0.0)
                else:
                    rest[g] = rest[g] - step * rest_row
                inv[g] = inv[g] - step * inv_row
                for q in range(j + 1, 8):
                    cols[q][g - b] = cols[q][g - b] - step * heads[q - j - 1]
                if g == b:
                    rest[g] = rest[g] - step * rest_row
        inv[b] = inv[b] * lax.rsqrt(pivots)
    return jnp.concatenate(inv, axis=0) if groups > 1 else inv[0]


def factor_step(image, size):
    inner = full_dot(image, image, (0, 0))
    return inverse_factor(inner[:size], size)


def orth(gram, basis, basis_t, size):
    def step(_, c):
        image = full_dot(gram[...], basis[...])
        lower = factor_step(image, size)
        basis[:, :size] = full_dot(image, lower, (1, 1))
        basis_t[...] = full_dot(lower, image, (1, 1))
        return c

    lax.fori_loop(0, ITERS, step, 0)


def swap(x):
    return pltpu.roll(x, 64, 1)


def regroup(a, b):
    left = lax.broadcasted_iota(jnp.int32, a.shape, 1) < 64
    return jnp.where(left, a, swap(b)), jnp.where(left, swap(a), b)


def main_kernel(
    x_hbm, start_f, start_s, start_r, start_c, rank_f, rank_s,
    mixed_out, frames_out,
    xin, xhi, xlo, acc, side, acc_s, side_s, gram, part_f, part_r, part_c,
    in_f, in_r, in_c, tot_f, tot_r, tot_c, bf, bft, bs, bst, br, brt, bc, bct,
    red, kron, send1, recv1, unf, send2, recv2,
    load_sems, sems, swap_sems,
):
    me = me_index()
    mine_row, mine_col = lax.axis_index("row"), lax.axis_index("col")
    for r in range(ROWS):
        pltpu.make_async_copy(x_hbm.at[r], xin.at[r], load_sems.at[r]).start()
    barrier = pltpu.get_barrier_semaphore()

    def greet(s, c):
        pl.semaphore_signal(barrier, inc=1, device_id=coords((me + s) % NDEV), device_id_type=MESH)
        return c

    lax.fori_loop(1, NDEV, greet, 0)

    acc[...] = jnp.zeros_like(acc)
    side[...] = jnp.zeros_like(side)
    acc_s[...] = jnp.zeros_like(acc_s)
    side_s[...] = jnp.zeros_like(side_s)
    for ref, start in ((bf, start_f), (br, start_r), (bc, start_c), (bs, start_s)):
        ref[...] = jnp.zeros_like(ref)
    bf[:, :TMAX] = start_f[...]
    bs[:NK, :KMAX] = start_s[...]
    rows_start = start_r[...].reshape(16, 2, 8, RS)
    br[:128, :RS] = rows_start[:, 0].reshape(128, RS)
    br[128:, :RS] = rows_start[:, 1].reshape(128, RS)
    bc[:, :RS] = start_c[...]

    def gather(r, c):
        pltpu.make_async_copy(x_hbm.at[r], xin.at[r], load_sems.at[r]).wait()
        hi, lo = halves(xin[r])
        xhi[r] = hi
        xlo[r] = lo
        acc[...] += dot(hi, hi, (0, 0))
        side[...] += dot(hi, lo, (0, 0))
        acc_s[...] += dot(hi[:256], hi[:256], (1, 1)) + dot(hi[256:], hi[256:], (1, 1))
        side_s[...] += dot(hi[:256], lo[:256], (1, 1)) + dot(hi[256:], lo[256:], (1, 1))
        return c

    lax.fori_loop(0, ROWS, gather, 0)
    pack(acc[...] + side[...] + side[...].T, part_f)
    sends = acc_s[...] + side_s[...] + side_s[...].T
    i0 = lax.broadcasted_iota(jnp.int32, (256, 256), 0)
    i1 = lax.broadcasted_iota(jnp.int32, (256, 256), 1)
    sends = jnp.where(i0 // NK == i1 // NK, sends, 0.0).reshape(16, NK, 256).sum(axis=0)
    j0 = lax.broadcasted_iota(jnp.int32, (256, 128), 0)
    j1 = lax.broadcasted_iota(jnp.int32, (256, 128), 1)
    part_f[48:50] = full_dot(sends, (j0 % NK == j1).astype(F32)).reshape(2, 8, 128)

    pl.semaphore_wait(barrier, NDEV - 1)
    all_sum(me, 50, part_f, in_f, tot_f, sems.at[0])

    unpack(tot_f, gram)

    def both(_, c):
        image = full_dot(gram[...], bf[...])
        small = full_dot(tot_f[48:50].reshape(NK, 128), bs[...])
        lower = factor_step(image, TMAX)
        lower_s = factor_step(small, KMAX)
        bf[:, :TMAX] = full_dot(image, lower, (1, 1))
        bft[...] = full_dot(lower, image, (1, 1))
        bs[:NK, :KMAX] = full_dot(small, lower_s, (1, 1))
        return c

    lax.fori_loop(0, ITERS, both, 0)
    keep_f = lax.broadcasted_iota(jnp.int32, (TMAX, NT), 0) < rank_f[0]
    frames_t = bft[...] * keep_f.astype(F32)
    frames_out[...] = frames_t
    keep_s = lax.broadcasted_iota(jnp.int32, (128, 128), 1) < rank_s[0]
    sends = bs[...] * keep_s.astype(F32)
    a0 = lax.broadcasted_iota(jnp.int32, (128, 256), 0)
    a1 = lax.broadcasted_iota(jnp.int32, (128, 256), 1)
    wide = full_dot(sends[:NK], (a0 == a1 // COLS).astype(F32))
    c0 = lax.broadcasted_iota(jnp.int32, (LINES, 256), 0)
    c1 = lax.broadcasted_iota(jnp.int32, (LINES, 256), 1)
    kron[...] = jnp.where(c0 // NK == c1 % COLS, jnp.concatenate([wide] * COLS, axis=0), 0.0)

    f_hi, f_lo = halves(frames_t)
    f_two = jnp.concatenate([f_hi, f_lo], axis=0)
    for r in range(ROWS):
        both_ways = dot(f_two, xhi[r], (1, 1))
        here = both_ways[:TMAX] + both_ways[TMAX:] + dot(f_hi, xlo[r], (1, 1))
        for q in range(4):
            red[q, pl.ds((r // 8) * 256 + r % 8, TMAX, stride=8), :] = here[:, 128 * q : 128 * q + 128]
    core = dot3(jnp.concatenate([red[q] for q in range(4)], axis=1), kron[...])
    for t in range(2):
        lanes = slice(128 * t, 128 * t + 128)
        one, two = regroup(core[:256, lanes], core[256:, lanes])
        send1[32 * t : 32 * t + 32] = one.reshape(32, 8, 128)
        send1[64 + 32 * t : 96 + 32 * t] = two.reshape(32, 8, 128)

    own = mine_col * 16 + mine_row
    recv1[own] = send1[me]

    def deal(s, c):
        dev = (me + s) % NDEV
        remote(send1.at[dev], recv1.at[own], swap_sems.at[0], swap_sems.at[1], dev).start()
        return c

    lax.fori_loop(1, NDEV, deal, 0)
    wait_for(recv1, NDEV - 1, swap_sems.at[1])

    for p in range(4):
        lanes = slice(128 * p, 128 * p + 128)
        one, two = regroup(
            recv1[32 * p : 32 * p + 16].reshape(128, 128), recv1[32 * p + 16 : 32 * p + 32].reshape(128, 128)
        )
        unf[:128, lanes] = one
        unf[128:, lanes] = two
    pack(self_dot(unf[...]), part_r)
    all_sum(me, 48, part_r, in_r, tot_r, sems.at[1])
    unpack(tot_r, gram)
    orth(gram, br, brt, RS)

    second = dot3(brt[...], unf[...])
    turned = second.T.reshape(8, 2, 32, RS)
    cols = [turned[:, e].reshape(256, RS) for e in range(2)]
    pack(self_dot(cols[0]) + self_dot(cols[1]), part_c)
    all_sum(me, 48, part_c, in_c, tot_c, sems.at[2])
    unpack(tot_c, gram)
    orth(gram, bc, bct, RS)

    backs = []
    for e in range(2):
        third = dot3(bct[...], cols[e])
        backs.append(dot3(bc[:, :RS], third).reshape(8, 1, 32, RS))
    back = jnp.concatenate(backs, axis=1).reshape(512, RS)
    projected = dot3(br[:, :RS], back, (1, 1))
    for p in range(4):
        lanes = slice(128 * p, 128 * p + 128)
        one, two = regroup(projected[:128, lanes], projected[128:, lanes])
        send2[32 * p : 32 * p + 16] = one.reshape(16, 8, 128)
        send2[32 * p + 16 : 32 * p + 32] = two.reshape(16, 8, 128)
    recv2[me] = send2[own]

    def hand_back(s, c):
        dev = (me + s) % NDEV
        place = (dev % 8) * 16 + dev // 8
        remote(send2.at[place], recv2.at[me], swap_sems.at[2], swap_sems.at[3], dev).start()
        return c

    lax.fori_loop(1, NDEV, hand_back, 0)
    wait_for(recv2, NDEV - 1, swap_sems.at[3])
    upper, lower = [], []
    for t in range(2):
        one, two = regroup(
            recv2[32 * t : 32 * t + 32].reshape(256, 128), recv2[64 + 32 * t : 96 + 32 * t].reshape(256, 128)
        )
        upper.append(one)
        lower.append(two)
    whole = jnp.concatenate([jnp.concatenate(upper, axis=1), jnp.concatenate(lower, axis=1)], axis=0)
    mixed_out[...] = dot3(whole, kron[...], (1, 1))
    wait_for(send1, NDEV - 1, swap_sems.at[0])
    wait_for(send2, NDEV - 1, swap_sems.at[2])


def last_kernel(x_ref, mixed, frames, out_ref):
    r = pl.program_id(0)
    m_hi, m_lo = halves(mixed[...])
    f_hi, f_lo = halves(frames[...])
    tall = jnp.concatenate([m_hi, m_lo, m_hi], axis=0)
    flat = jnp.concatenate([f_hi, f_hi, f_lo], axis=0)
    out_ref[0] = x_ref[0] - dot(tall, flat, (0, 0))


def local(signal, start_frames, start_sends, start_rows, start_cols, rank_frames, rank_sends):
    x = signal.reshape(ROWS, LINES, NT)
    vmem = pl.BlockSpec(memory_space=pltpu.VMEM)
    smem = pl.BlockSpec(memory_space=pltpu.SMEM)
    tiles = lambda n: pltpu.VMEM((n, 8, 128), F32)
    flat = lambda *dims: pltpu.VMEM(dims, F32)
    mixed, frames = pl.pallas_call(
        main_kernel,
        out_shape=(jax.ShapeDtypeStruct((512, 512), F32), jax.ShapeDtypeStruct((TMAX, NT), F32)),
        in_specs=[pl.BlockSpec(memory_space=pl.ANY), vmem, vmem, vmem, vmem, smem, smem],
        out_specs=(vmem, vmem),
        scratch_shapes=[
            flat(ROWS, LINES, NT), pltpu.VMEM((ROWS, LINES, NT), BF16), pltpu.VMEM((ROWS, LINES, NT), BF16),
            flat(256, 256), flat(256, 256), flat(256, 256), flat(256, 256), flat(256, 256),
            tiles(50), tiles(48), tiles(48), tiles(NDEV - 1), tiles(NDEV - 1), tiles(NDEV - 1),
            tiles(50), tiles(48), tiles(48),
            flat(256, 128), flat(TMAX, 256), flat(128, 128), flat(8, 128),
            flat(256, 128), flat(RS, 256), flat(256, 128), flat(RS, 256),
            flat(4, 512, 128), flat(512, 256), tiles(NDEV), tiles(NDEV), flat(256, 512), tiles(NDEV), tiles(NDEV),
            pltpu.SemaphoreType.DMA((ROWS,)), pltpu.SemaphoreType.DMA((3, 4)), pltpu.SemaphoreType.DMA((4,)),
        ],
        compiler_params=pltpu.CompilerParams(
            collective_id=1, has_side_effects=True, vmem_limit_bytes=56 * 1024 * 1024
        ),
        name="modes",
    )(x, start_frames, start_sends, start_rows, start_cols, rank_frames, rank_sends)
    mixed = mixed.reshape(2, TMAX, 8, LINES).transpose(0, 2, 1, 3).reshape(512, 512)
    out = pl.pallas_call(
        last_kernel,
        grid=(ROWS,),
        out_shape=jax.ShapeDtypeStruct(x.shape, F32),
        in_specs=[
            pl.BlockSpec((1, LINES, NT), lambda r: (r, 0, 0)),
            pl.BlockSpec((TMAX, LINES), lambda r: (r, 0)),
            pl.BlockSpec((TMAX, NT), lambda r: (0, 0)),
        ],
        out_specs=pl.BlockSpec((1, LINES, NT), lambda r: (r, 0, 0)),
        compiler_params=pltpu.CompilerParams(dimension_semantics=("arbitrary",)),
        name="subtract",
    )(x, mixed, frames)
    return out.reshape(signal.shape)


def solution(mesh):
    return jax.shard_map(
        local,
        mesh=mesh,
        in_specs=(P("row", "col", None, None), P(), P(), P(), P(), P(), P()),
        out_specs=P("row", "col", None, None),
        check_vma=False,
    )
```

time: 287 us -> 134 us (0.47); the launches traced: 283 us -> 133 us
  other arithmetic: 72.9 us -> 0 us
  matrix products: 62.4 us -> 0 us
  Pallas kernels: 72.8 us -> 123 us
  blocking collectives: 38.8 us -> 0 us
  local copies, waits for them, and re-layouts: 34.1 us -> 8.91 us
    another operation x40 -> x0, other arithmetic: 67 us -> none  [the longest x24 36.1 us: orthonormal(): factor = jnp.linalg.cholesky(inner)]
    dot_general x28 -> x0, matrix products: 60.4 us -> none  [the longest x1 14.9 us: local(): local_sends = jnp.einsum('pkt,pjt->kj', blocks, blocks, precision=high)]
    pallas_call x3 -> x2, Pallas kernels: 72.8 us -> 123 us  [the longest x1 109 us: local(): pl.pallas_call(main_kernel, out_shape=(jax.ShapeDtypeStruct((512, 512), F...]
    all_to_all x2 -> x0, blocking collectives: 38.8 us -> none  [the longest x1 19.7 us: local(): spread = lax.all_to_all(parts, ('row', 'col'), 0, 0, tiled=True)]
    reshape x11 -> x1, local copies, waits for them, and re-layouts: 13.4 us -> 2.87 us  [local(): mixed.reshape(2, TMAX, 8, LINES).transpose(0, 2, 1, 3).reshape(512, 512)]
    dot_general x12 -> x0, local copies, waits for them, and re-layouts: 7.54 us -> none  [the longest x1 3.84 us: local(): jnp.dot(expanded.reshape(-1, TMAX), basis_frames.T, precision=high)]
    another operation x2 -> x0, local copies, waits for them, and re-layouts: 4.06 us -> none  [the longest x1 3.52 us: local(): unfolded = spread.reshape(256, -1)]
    all_to_all x2 -> x0, other arithmetic: 3.72 us -> none  [the longest x1 1.86 us: local(): back = lax.all_to_all(parts, ('row', 'col'), 0, 0, tiled=True)]
where the time goes in v2:
time: 134 us; the launch traced here: 133 us
  Pallas kernels  123 us (92%)
  local copies, waits for them, and re-layouts  8.91 us (7%)
    pallas_call x1, Pallas kernels, local(): pl.pallas_call(main_kernel, out_shape=(jax.ShapeDtypeStruct((512, 512), F...  109 us
    pallas_call x1, Pallas kernels, local(): pl.pallas_call(last_kernel, grid=(ROWS,), out_shape=jax.ShapeDtypeStruct(...  13.7 us
    unnamed x4, local copies, waits for them, and re-layouts  6.05 us
    reshape x1, local copies, waits for them, and re-layouts, local(): mixed.reshape(2, TMAX, 8, LINES).transpose(0, 2, 1, 3).reshape(512, 512)  2.87 us

profile of v2, /device:TPU:1, one launch (start us, length us, event | category | flops | bytes accessed | tf_op | source)
XLA Modules:
  0.0 132.9 jit_solution(9255104200920060835)
XLA Ops:
  1.3 1.3 %copy.9.start_s = f32[16,8]{1,0:T(8,128)} copy(f32[16,8]{0,1:T(8,128)} %param.9) | data formatting | bytes 1024 | tf_op args[2]
  2.6 1.5 %copy.8.start_f = f32[256,32]{1,0:T(8,128)} copy(f32[256,32]{0,1:T(8,128)} %param.8) | data formatting | bytes 65536 | tf_op args[1]
  4.2 1.6 %copy.10.start_r = f32[256,64]{1,0:T(8,128)} copy(f32[256,64]{0,1:T(8,128)} %param.10) | data formatting | bytes 131072 | tf_op args[3]
  5.7 1.6 %copy.11.start_c = f32[256,64]{1,0:T(8,128)} copy(f32[256,64]{0,1:T(8,128)} %param.11) | data formatting | bytes 131072 | tf_op args[4]
  7.3 109.0 %modes.1 = (f32[512,512]{1,0:T(8,128)}, f32[32,256]{1,0:T(8,128)}) custom-call(f32[16,512,256]{2,1,0:T(8,128)} %bitcast.6, f32[256,32]{1,0:T(8,128)} %copy.8.start_f, f32[16,8]{1,0:T(8,128)} %copy.9.start_s, f32[256,64]{1,0:T(8,128)} %copy.10.start_r, f32[256,64]{1,0:T(8,128)} %copy.11.start_c, s32[1]{0:T(128)S(6)} %copy.13.rank_f, s32[1]{0:T(128)S(6)} %copy.14.rank_s), custom_call_target="tpu_custom_call" | custom-call | tf_op jit(solution)/shard_map/modes/pallas_call | solution.py:367
  116.4 2.9 %copy.12 = f32[2,32,8,512]{3,1,2,0:T(8,128)} copy(f32[2,32,8,512]{3,2,1,0:T(8,128)} %bitcast.9) | data formatting | bytes 2097152 | tf_op jit(solution)/shard_map/reshape | solution.py:387
  119.3 13.7 %subtract.1 = f32[16,512,256]{2,1,0:T(8,128)} custom-call(f32[16,512,256]{2,1,0:T(8,128)} %bitcast.7, f32[512,512]{1,0:T(8,128)} %bitcast.8, f32[32,256]{1,0:T(8,128)} %get-tuple-element.8.frames), custom_call_target="tpu_custom_call" | custom-call | tf_op jit(solution)/shard_map/subtract/pallas_call | solution.py:388
